TPU v7x, 32 devices: a whole 2x2x4 slice. The times are simulated.
32 devices in a mesh: atoms: 16 (over z, y, x), vecs: 2 (over core).
Axes of the slice: x: 2, y: 2, z: 4, core: 2. Of those that a mesh axis runs over, the one named last changes fastest.
Arguments:
- start_block: bfloat16 [8192, 1024], P('atoms', 'vecs'), may hold values from -6 to 6
- onsite: bfloat16 [64, 128, 128], P('atoms'), may hold values from -0.15625 to 0.15625
- hopping: bfloat16 [64, 4, 128, 128], P('atoms'), as said below
- columns: int32 [64, 4], P('atoms'), may hold values from 0 to 63, as said below
- counts: int32 [64], P('atoms'), may hold values from 0 to 4, as said below
Outputs:
- filtered: bfloat16 [8192, 1024], P('atoms', 'vecs')
- gram: float32 [1024, 1024], P('atoms', 'vecs')
- projected: float32 [1024, 1024], P('atoms', 'vecs')
Inputs may be any that keep to these rules, and one draw needn't show every extreme that they name: `columns`: each block row lists its live neighbours in its first counts[i] slots; every neighbour lies at most 2 blocks away, counted cyclically over the 64 blocks; the neighbour relation is symmetric; the other slots name blocks within the same reach that are not neighbours. `counts`: some block row has all 4 slots live. For a live slot, hopping[j, t] with columns[j, t] = i is the transpose of hopping[i, s] with columns[i, s] = j.
All inputs are finite; a program needn't handle non-finite values.
Results may differ from a plain program's by a relative error of at most 0.0098.
Values may be sent and summed in bfloat16 or wider, within the bound.
A program may use at most 64 MiB of HBM per device.

v0:
```python
import jax
import jax.numpy as jnp
from jax import lax
from jax.sharding import PartitionSpec as P

DEG = 12


filter_low = -0.5
filter_top = 4.0
filter_bottom = -1.6


def padded(cells, sides, width):
    for axis, dim in sides:
        count = lax.axis_size(axis)
        head = lax.slice_in_dim(cells, 0, width, axis=dim)
        tail = lax.slice_in_dim(cells, cells.shape[dim] - width, cells.shape[dim], axis=dim)
        cells = jnp.concatenate(
            [
                lax.ppermute(tail, axis, [(i, (i + 1) % count) for i in range(count)]),
                cells,
                lax.ppermute(head, axis, [((i + 1) % count, i) for i in range(count)]),
            ],
            axis=dim,
        )
    return cells


def filter_coefficients(degree):
    center = 0.5 * (filter_top + filter_low)
    half_width = 0.5 * (filter_top - filter_low)
    sigma_first = half_width / (filter_bottom - center)
    listed = [(sigma_first / half_width, 0.0)]
    sigma_now = sigma_first
    for degree_step in range(1, degree):
        sigma_next = 1.0 / (2.0 / sigma_first - sigma_now)
        listed.append((2.0 * sigma_next / half_width, sigma_now * sigma_next))
        sigma_now = sigma_next
    return (center, listed)


def hop_apply(
    window, base_block, onsite_rows, hopping_rows, column_rows, count_rows, offset, total_blocks
):
    row_count = onsite_rows.shape[0]
    slot_count = column_rows.shape[1]
    local_index = jnp.mod(column_rows - base_block, total_blocks)
    live_slot = jnp.arange(slot_count, dtype=jnp.int32)[None, :] < count_rows[:, None]
    masked = jnp.where(live_slot[:, :, None, None], hopping_rows, jnp.zeros((), jnp.bfloat16))
    picked = window[local_index]
    summed = jnp.einsum("rsij,rsjc->ric", masked, picked, preferred_element_type=jnp.float32)
    own_rows = window[offset : offset + row_count]
    direct = jnp.einsum("rij,rjc->ric", onsite_rows, own_rows, preferred_element_type=jnp.float32)
    mirrored = jnp.einsum("rji,rjc->ric", onsite_rows, own_rows, preferred_element_type=jnp.float32)
    return summed + 0.5 * (direct + mirrored)


def shards(start_block, onsite, hopping, columns, counts):
    blocks_dev = onsite.shape[0]
    block_rows = onsite.shape[1]
    reach_blocks = columns.shape[1] // 2
    width_dev = start_block.shape[1]
    total_blocks = blocks_dev * lax.axis_size("atoms")
    first_block = lax.axis_index("atoms") * blocks_dev
    center, listed = filter_coefficients(DEG)
    scale_table = jnp.array([pair[0] for pair in listed], jnp.float32)
    carry_table = jnp.array([pair[1] for pair in listed], jnp.float32)

    def apply_own(current):
        flat_rows = current.reshape(blocks_dev * block_rows, width_dev)
        rimmed = padded(flat_rows, (("atoms", 0),), reach_blocks * block_rows)
        rimmed = rimmed.reshape(blocks_dev + 2 * reach_blocks, block_rows, width_dev)
        return hop_apply(
            rimmed,
            first_block - reach_blocks,
            onsite,
            hopping,
            columns,
            counts,
            reach_blocks,
            total_blocks,
        )

    start_rows = start_block.reshape(blocks_dev, block_rows, width_dev)
    zero_rows = jnp.zeros_like(start_rows)

    def one_step(step_index, state):
        current, previous = state
        applied = apply_own(current)
        following = scale_table[step_index] * (
            applied - center * current.astype(jnp.float32)
        ) - carry_table[step_index] * previous.astype(jnp.float32)
        return (following.astype(jnp.bfloat16), current)

    final_rows, unused_rows = lax.fori_loop(0, DEG, one_step, (start_rows, zero_rows))
    filtered = final_rows.reshape(blocks_dev * block_rows, width_dev)
    applied_final = (
        apply_own(final_rows).astype(jnp.bfloat16).reshape(blocks_dev * block_rows, width_dev)
    )
    full_block = lax.all_gather(filtered, "vecs", axis=1, tiled=True)
    gram_part = lax.dot_general(
        full_block, filtered, (((0,), (0,)), ((), ())), preferred_element_type=jnp.float32
    )
    projected_part = lax.dot_general(
        full_block, applied_final, (((0,), (0,)), ((), ())), preferred_element_type=jnp.float32
    )
    summed = lax.psum_scatter(
        jnp.stack([gram_part, projected_part], axis=1), "atoms", scatter_dimension=0, tiled=True
    )
    total_rows = total_blocks * block_rows
    gram = summed[:, 0] / total_rows
    projected = summed[:, 1] / total_rows
    return (filtered, gram, projected)


def solution(mesh):
    in_specs = (
        P("atoms", "vecs"),
        P("atoms", None, None),
        P("atoms", None, None, None),
        P("atoms", None),
        P("atoms"),
    )
    out_specs = (P("atoms", "vecs"), P("atoms", "vecs"), P("atoms", "vecs"))
    return jax.shard_map(shards, mesh=mesh, in_specs=in_specs, out_specs=out_specs, check_vma=False)
```

profile of v0, /device:TPU:1, one launch (start us, length us, event | category | flops | bytes accessed | tf_op | source)
XLA Modules:
  0.0 389.7 jit_solution(7116892120469375574)
XLA Ops:
  10.1 251.0 %while.18 = (s32[]{:T(128)}, bf16[4,128,512]{2,1,0:T(8,128)(2,1)S(1)}, bf16[4,128,512]{2,1,0:T(8,128)(2,1)}, s32[4]{0:T(128)}, bf16[4,4,128,128]{3,2,1,0:T(8,128...) while((s32[]{:T(128)}, ...), condition=%wide.region_1.2_spmd.clone, body=%wide.region_0.1_spmd.sunk.clone.sunk | while | flops 408945920 | bytes 29102828 | solution.py:96
  10.2 2.1 collective-permute-start.1
  12.2 4.1 %collective-permute-start = (bf16[256,512]{1,0:T(8,128)(2,1)S(1)}, bf16[256,512]{1,0:T(8,128)(2,1)S(1)}, u32[]{:S(2)}, u32[]{:S(2)}) collective-permute-start(bf16[256,512]{1,0:T(8,128)(2,1)S(1)} %bitcast.92), channel_id=1, source_target_pairs={{2,0},{4,2},{6,4},{8,6},{10,8},{12,10},{14,12},{16,14},{18,16},{20... | collective-permute-start | bytes 786440 | tf_op jit(solution)/shard_map/while/body/eval_jaxpr/ppermute | solution.py:23
  22.9 1.9 collective-permute-done
  25.8 2.0 gather_fusion
  33.0 3.9 collective-permute-start
  42.6 1.8 collective-permute-done
  45.4 2.0 gather_fusion
  51.9 4.9 %collective-permute-start = (bf16[256,512]{1,0:T(8,128)(2,1)S(1)}, bf16[256,512]{1,0:T(8,128)(2,1)S(1)}, u32[]{:S(2)}, u32[]{:S(2)}) collective-permute-start(bf16[256,512]{1,0:T(8,128)(2,1)S(1)} %bitcast.92), channel_id=1, source_target_pairs={{2,0},{4,2},{6,4},{8,6},{10,8},{12,10},{14,12},{16,14},{18,16},{20... | collective-permute-start | bytes 786440 | tf_op jit(solution)/shard_map/while/body/eval_jaxpr/ppermute | solution.py:23
  62.2 2.0 collective-permute-done
  65.2 2.0 gather_fusion
  68.6 1.7 fusion.57
  71.4 5.4 %collective-permute-start = (bf16[256,512]{1,0:T(8,128)(2,1)S(1)}, bf16[256,512]{1,0:T(8,128)(2,1)S(1)}, u32[]{:S(2)}, u32[]{:S(2)}) collective-permute-start(bf16[256,512]{1,0:T(8,128)(2,1)S(1)} %bitcast.92), channel_id=1, source_target_pairs={{2,0},{4,2},{6,4},{8,6},{10,8},{12,10},{14,12},{16,14},{18,16},{20... | collective-permute-start | bytes 786440 | tf_op jit(solution)/shard_map/while/body/eval_jaxpr/ppermute | solution.py:23
  82.2 6.9 %collective-permute-done = bf16[256,512]{1,0:T(8,128)(2,1)S(1)} collective-permute-done((bf16[256,512]{1,0:T(8,128)(2,1)S(1)}, bf16[256,512]{1,0:T(8,128)(2,1)S(1)}, u32[]{:S(2)}, u32[]{:S(2)}) %collective-permute-start) | collective-permute-done | bytes 262176 | tf_op jit(solution)/shard_map/while/body/eval_jaxpr/ppermute | solution.py:23
  90.1 2.0 gather_fusion
  96.4 4.8 %collective-permute-start = (bf16[256,512]{1,0:T(8,128)(2,1)S(1)}, bf16[256,512]{1,0:T(8,128)(2,1)S(1)}, u32[]{:S(2)}, u32[]{:S(2)}) collective-permute-start(bf16[256,512]{1,0:T(8,128)(2,1)S(1)} %bitcast.92), channel_id=1, source_target_pairs={{2,0},{4,2},{6,4},{8,6},{10,8},{12,10},{14,12},{16,14},{18,16},{20... | collective-permute-start | bytes 786440 | tf_op jit(solution)/shard_map/while/body/eval_jaxpr/ppermute | solution.py:23
  106.5 2.6 collective-permute-done
  110.2 2.0 gather_fusion
  116.4 4.8 %collective-permute-start = (bf16[256,512]{1,0:T(8,128)(2,1)S(1)}, bf16[256,512]{1,0:T(8,128)(2,1)S(1)}, u32[]{:S(2)}, u32[]{:S(2)}) collective-permute-start(bf16[256,512]{1,0:T(8,128)(2,1)S(1)} %bitcast.92), channel_id=1, source_target_pairs={{2,0},{4,2},{6,4},{8,6},{10,8},{12,10},{14,12},{16,14},{18,16},{20... | collective-permute-start | bytes 786440 | tf_op jit(solution)/shard_map/while/body/eval_jaxpr/ppermute | solution.py:23
  126.6 2.4 collective-permute-done
  130.0 2.0 gather_fusion
  136.3 4.8 %collective-permute-start = (bf16[256,512]{1,0:T(8,128)(2,1)S(1)}, bf16[256,512]{1,0:T(8,128)(2,1)S(1)}, u32[]{:S(2)}, u32[]{:S(2)}) collective-permute-start(bf16[256,512]{1,0:T(8,128)(2,1)S(1)} %bitcast.92), channel_id=1, source_target_pairs={{2,0},{4,2},{6,4},{8,6},{10,8},{12,10},{14,12},{16,14},{18,16},{20... | collective-permute-start | bytes 786440 | tf_op jit(solution)/shard_map/while/body/eval_jaxpr/ppermute | solution.py:23
  146.4 4.8 %collective-permute-done = bf16[256,512]{1,0:T(8,128)(2,1)S(1)} collective-permute-done((bf16[256,512]{1,0:T(8,128)(2,1)S(1)}, bf16[256,512]{1,0:T(8,128)(2,1)S(1)}, u32[]{:S(2)}, u32[]{:S(2)}) %collective-permute-start) | collective-permute-done | bytes 262176 | tf_op jit(solution)/shard_map/while/body/eval_jaxpr/ppermute | solution.py:23
  152.3 2.0 gather_fusion
  158.5 4.8 %collective-permute-start = (bf16[256,512]{1,0:T(8,128)(2,1)S(1)}, bf16[256,512]{1,0:T(8,128)(2,1)S(1)}, u32[]{:S(2)}, u32[]{:S(2)}) collective-permute-start(bf16[256,512]{1,0:T(8,128)(2,1)S(1)} %bitcast.92), channel_id=1, source_target_pairs={{2,0},{4,2},{6,4},{8,6},{10,8},{12,10},{14,12},{16,14},{18,16},{20... | collective-permute-start | bytes 786440 | tf_op jit(solution)/shard_map/while/body/eval_jaxpr/ppermute | solution.py:23
  168.6 4.5 %collective-permute-done = bf16[256,512]{1,0:T(8,128)(2,1)S(1)} collective-permute-done((bf16[256,512]{1,0:T(8,128)(2,1)S(1)}, bf16[256,512]{1,0:T(8,128)(2,1)S(1)}, u32[]{:S(2)}, u32[]{:S(2)}) %collective-permute-start) | collective-permute-done | bytes 262176 | tf_op jit(solution)/shard_map/while/body/eval_jaxpr/ppermute | solution.py:23
  174.2 2.0 gather_fusion
  180.5 4.8 %collective-permute-start = (bf16[256,512]{1,0:T(8,128)(2,1)S(1)}, bf16[256,512]{1,0:T(8,128)(2,1)S(1)}, u32[]{:S(2)}, u32[]{:S(2)}) collective-permute-start(bf16[256,512]{1,0:T(8,128)(2,1)S(1)} %bitcast.92), channel_id=1, source_target_pairs={{2,0},{4,2},{6,4},{8,6},{10,8},{12,10},{14,12},{16,14},{18,16},{20... | collective-permute-start | bytes 786440 | tf_op jit(solution)/shard_map/while/body/eval_jaxpr/ppermute | solution.py:23
  190.6 4.3 %collective-permute-done = bf16[256,512]{1,0:T(8,128)(2,1)S(1)} collective-permute-done((bf16[256,512]{1,0:T(8,128)(2,1)S(1)}, bf16[256,512]{1,0:T(8,128)(2,1)S(1)}, u32[]{:S(2)}, u32[]{:S(2)}) %collective-permute-start) | collective-permute-done | bytes 262176 | tf_op jit(solution)/shard_map/while/body/eval_jaxpr/ppermute | solution.py:23
  195.9 2.0 gather_fusion
  202.2 4.8 %collective-permute-start = (bf16[256,512]{1,0:T(8,128)(2,1)S(1)}, bf16[256,512]{1,0:T(8,128)(2,1)S(1)}, u32[]{:S(2)}, u32[]{:S(2)}) collective-permute-start(bf16[256,512]{1,0:T(8,128)(2,1)S(1)} %bitcast.92), channel_id=1, source_target_pairs={{2,0},{4,2},{6,4},{8,6},{10,8},{12,10},{14,12},{16,14},{18,16},{20... | collective-permute-start | bytes 786440 | tf_op jit(solution)/shard_map/while/body/eval_jaxpr/ppermute | solution.py:23
  214.9 2.0 gather_fusion
  218.3 1.7 fusion.57
  220.8 1.9 collective-permute-start.1
  222.7 3.2 collective-permute-start
  231.3 1.9 collective-permute-done.1
  234.3 2.0 gather_fusion
  240.2 2.3 collective-permute-start.1
  242.5 2.9 collective-permute-start
  252.1 2.1 collective-permute-done
  255.3 2.0 gather_fusion
  266.2 2.4 fusion.25
  268.5 7.6 %collective-permute-done.2 = bf16[256,512]{1,0:T(8,128)(2,1)S(1)} collective-permute-done((bf16[256,512]{1,0:T(8,128)(2,1)S(1)}, bf16[256,512]{1,0:T(8,128)(2,1)S(1)}, u32[]{:S(2)}, u32[]{:S(2)}) %collective-permute-start.2) | collective-permute-done | bytes 262176 | tf_op jit(solution)/shard_map/ppermute | solution.py:21
  277.2 2.0 gather_fusion.1
  280.7 2.1 convolution_bitcast_fusion.2
  283.5 2.4 pad_maximum_fusion.1
  285.9 95.3 %reduce-scatter.2.cloned.1.call-done = f32[64,2,512]{2,0,1:T(8,128)} async-done(((f32[1024,2,512]{2,0,1:T(8,128)}), f32[64,2,512]{2,0,1:T(8,128)}) %reduce-scatter.2.cloned.1.call-update) | async-done | bytes 262160 | tf_op jit(solution)/shard_map/reduce_scatter | solution.py:108
  381.2 1.7 fusion.18
  (280 shorter events, 140.1 us)
Async XLA Ops:
  7.2 273.5 %all-gather.2.cloned.1.call-start = ((), (), s32[]{:S(2)}) async-start(), calls=%async_computation.1 | async-start | bytes 1572864 | tf_op jit(solution)/shard_map/all_gather | solution.py:101
  10.1 256.0 %copy-start.8 = (bf16[4,128,128]{2,1,0:T(8,128)(2,1)S(1)}, bf16[4,128,128]{2,1,0:T(8,128)(2,1)}, u32[]{:S(2)}) copy-start(bf16[4,128,128]{2,1,0:T(8,128)(2,1)} %param.10) | copy-start | bytes 393220
  10.2 12.7 %collective-permute-start.1 = (bf16[256,512]{1,0:T(8,128)(2,1)S(1)}, bf16[256,512]{1,0:T(8,128)(2,1)S(1)}, u32[]{:S(2)}, u32[]{:S(2)}) collective-permute-start(bf16[256,512]{1,0:T(8,128)(2,1)S(1)} %bitcast.93), channel_id=1, source_target_pairs={{0,2},{2,4},{4,6},{6,8},{8,10},{10,12},{12,14},{14,16},{16,18},{18... | collective-permute-start | bytes 786440 | tf_op jit(solution)/shard_map/while/body/eval_jaxpr/ppermute | solution.py:21
  12.2 12.6 %collective-permute-start = (bf16[256,512]{1,0:T(8,128)(2,1)S(1)}, bf16[256,512]{1,0:T(8,128)(2,1)S(1)}, u32[]{:S(2)}, u32[]{:S(2)}) collective-permute-start(bf16[256,512]{1,0:T(8,128)(2,1)S(1)} %bitcast.92), channel_id=1, source_target_pairs={{2,0},{4,2},{6,4},{8,6},{10,8},{12,10},{14,12},{16,14},{18,16},{20... | collective-permute-start | bytes 786440 | tf_op jit(solution)/shard_map/while/body/eval_jaxpr/ppermute | solution.py:23
  25.8 2.0 copy-start.3
  27.8 1.3 copy-start.5
  31.7 10.9 %collective-permute-start.1 = (bf16[256,512]{1,0:T(8,128)(2,1)S(1)}, bf16[256,512]{1,0:T(8,128)(2,1)S(1)}, u32[]{:S(2)}, u32[]{:S(2)}) collective-permute-start(bf16[256,512]{1,0:T(8,128)(2,1)S(1)} %bitcast.93), channel_id=1, source_target_pairs={{0,2},{2,4},{4,6},{6,8},{8,10},{10,12},{12,14},{14,16},{16,18},{18... | collective-permute-start | bytes 786440 | tf_op jit(solution)/shard_map/while/body/eval_jaxpr/ppermute | solution.py:21
  33.0 11.4 %collective-permute-start = (bf16[256,512]{1,0:T(8,128)(2,1)S(1)}, bf16[256,512]{1,0:T(8,128)(2,1)S(1)}, u32[]{:S(2)}, u32[]{:S(2)}) collective-permute-start(bf16[256,512]{1,0:T(8,128)(2,1)S(1)} %bitcast.92), channel_id=1, source_target_pairs={{2,0},{4,2},{6,4},{8,6},{10,8},{12,10},{14,12},{16,14},{18,16},{20... | collective-permute-start | bytes 786440 | tf_op jit(solution)/shard_map/while/body/eval_jaxpr/ppermute | solution.py:23
  45.4 2.0 copy-start.3
  47.4 1.3 copy-start.5
  51.3 10.8 %collective-permute-start.1 = (bf16[256,512]{1,0:T(8,128)(2,1)S(1)}, bf16[256,512]{1,0:T(8,128)(2,1)S(1)}, u32[]{:S(2)}, u32[]{:S(2)}) collective-permute-start(bf16[256,512]{1,0:T(8,128)(2,1)S(1)} %bitcast.93), channel_id=1, source_target_pairs={{0,2},{2,4},{4,6},{6,8},{8,10},{10,12},{12,14},{14,16},{16,18},{18... | collective-permute-start | bytes 786440 | tf_op jit(solution)/shard_map/while/body/eval_jaxpr/ppermute | solution.py:21
  51.9 12.2 %collective-permute-start = (bf16[256,512]{1,0:T(8,128)(2,1)S(1)}, bf16[256,512]{1,0:T(8,128)(2,1)S(1)}, u32[]{:S(2)}, u32[]{:S(2)}) collective-permute-start(bf16[256,512]{1,0:T(8,128)(2,1)S(1)} %bitcast.92), channel_id=1, source_target_pairs={{2,0},{4,2},{6,4},{8,6},{10,8},{12,10},{14,12},{16,14},{18,16},{20... | collective-permute-start | bytes 786440 | tf_op jit(solution)/shard_map/while/body/eval_jaxpr/ppermute | solution.py:23
  65.2 2.0 copy-start.3
  67.2 1.3 copy-start.5
  71.1 11.1 %collective-permute-start.1 = (bf16[256,512]{1,0:T(8,128)(2,1)S(1)}, bf16[256,512]{1,0:T(8,128)(2,1)S(1)}, u32[]{:S(2)}, u32[]{:S(2)}) collective-permute-start(bf16[256,512]{1,0:T(8,128)(2,1)S(1)} %bitcast.93), channel_id=1, source_target_pairs={{0,2},{2,4},{4,6},{6,8},{8,10},{10,12},{12,14},{14,16},{16,18},{18... | collective-permute-start | bytes 786440 | tf_op jit(solution)/shard_map/while/body/eval_jaxpr/ppermute | solution.py:21
  71.4 17.6 %collective-permute-start = (bf16[256,512]{1,0:T(8,128)(2,1)S(1)}, bf16[256,512]{1,0:T(8,128)(2,1)S(1)}, u32[]{:S(2)}, u32[]{:S(2)}) collective-permute-start(bf16[256,512]{1,0:T(8,128)(2,1)S(1)} %bitcast.92), channel_id=1, source_target_pairs={{2,0},{4,2},{6,4},{8,6},{10,8},{12,10},{14,12},{16,14},{18,16},{20... | collective-permute-start | bytes 786440 | tf_op jit(solution)/shard_map/while/body/eval_jaxpr/ppermute | solution.py:23
  90.1 2.0 copy-start.3
  92.1 1.3 copy-start.5
  96.0 10.5 %collective-permute-start.1 = (bf16[256,512]{1,0:T(8,128)(2,1)S(1)}, bf16[256,512]{1,0:T(8,128)(2,1)S(1)}, u32[]{:S(2)}, u32[]{:S(2)}) collective-permute-start(bf16[256,512]{1,0:T(8,128)(2,1)S(1)} %bitcast.93), channel_id=1, source_target_pairs={{0,2},{2,4},{4,6},{6,8},{8,10},{10,12},{12,14},{14,16},{16,18},{18... | collective-permute-start | bytes 786440 | tf_op jit(solution)/shard_map/while/body/eval_jaxpr/ppermute | solution.py:21
  96.4 12.8 %collective-permute-start = (bf16[256,512]{1,0:T(8,128)(2,1)S(1)}, bf16[256,512]{1,0:T(8,128)(2,1)S(1)}, u32[]{:S(2)}, u32[]{:S(2)}) collective-permute-start(bf16[256,512]{1,0:T(8,128)(2,1)S(1)} %bitcast.92), channel_id=1, source_target_pairs={{2,0},{4,2},{6,4},{8,6},{10,8},{12,10},{14,12},{16,14},{18,16},{20... | collective-permute-start | bytes 786440 | tf_op jit(solution)/shard_map/while/body/eval_jaxpr/ppermute | solution.py:23
  110.2 2.0 copy-start.3
  116.1 10.5 %collective-permute-start.1 = (bf16[256,512]{1,0:T(8,128)(2,1)S(1)}, bf16[256,512]{1,0:T(8,128)(2,1)S(1)}, u32[]{:S(2)}, u32[]{:S(2)}) collective-permute-start(bf16[256,512]{1,0:T(8,128)(2,1)S(1)} %bitcast.93), channel_id=1, source_target_pairs={{0,2},{2,4},{4,6},{6,8},{8,10},{10,12},{12,14},{14,16},{16,18},{18... | collective-permute-start | bytes 786440 | tf_op jit(solution)/shard_map/while/body/eval_jaxpr/ppermute | solution.py:21
  116.4 12.6 %collective-permute-start = (bf16[256,512]{1,0:T(8,128)(2,1)S(1)}, bf16[256,512]{1,0:T(8,128)(2,1)S(1)}, u32[]{:S(2)}, u32[]{:S(2)}) collective-permute-start(bf16[256,512]{1,0:T(8,128)(2,1)S(1)} %bitcast.92), channel_id=1, source_target_pairs={{2,0},{4,2},{6,4},{8,6},{10,8},{12,10},{14,12},{16,14},{18,16},{20... | collective-permute-start | bytes 786440 | tf_op jit(solution)/shard_map/while/body/eval_jaxpr/ppermute | solution.py:23
  130.0 2.0 copy-start.3
  135.9 10.5 %collective-permute-start.1 = (bf16[256,512]{1,0:T(8,128)(2,1)S(1)}, bf16[256,512]{1,0:T(8,128)(2,1)S(1)}, u32[]{:S(2)}, u32[]{:S(2)}) collective-permute-start(bf16[256,512]{1,0:T(8,128)(2,1)S(1)} %bitcast.93), channel_id=1, source_target_pairs={{0,2},{2,4},{4,6},{6,8},{8,10},{10,12},{12,14},{14,16},{16,18},{18... | collective-permute-start | bytes 786440 | tf_op jit(solution)/shard_map/while/body/eval_jaxpr/ppermute | solution.py:21
  136.3 14.9 %collective-permute-start = (bf16[256,512]{1,0:T(8,128)(2,1)S(1)}, bf16[256,512]{1,0:T(8,128)(2,1)S(1)}, u32[]{:S(2)}, u32[]{:S(2)}) collective-permute-start(bf16[256,512]{1,0:T(8,128)(2,1)S(1)} %bitcast.92), channel_id=1, source_target_pairs={{2,0},{4,2},{6,4},{8,6},{10,8},{12,10},{14,12},{16,14},{18,16},{20... | collective-permute-start | bytes 786440 | tf_op jit(solution)/shard_map/while/body/eval_jaxpr/ppermute | solution.py:23
  152.3 2.0 copy-start.3
  158.1 10.5 %collective-permute-start.1 = (bf16[256,512]{1,0:T(8,128)(2,1)S(1)}, bf16[256,512]{1,0:T(8,128)(2,1)S(1)}, u32[]{:S(2)}, u32[]{:S(2)}) collective-permute-start(bf16[256,512]{1,0:T(8,128)(2,1)S(1)} %bitcast.93), channel_id=1, source_target_pairs={{0,2},{2,4},{4,6},{6,8},{8,10},{10,12},{12,14},{14,16},{16,18},{18... | collective-permute-start | bytes 786440 | tf_op jit(solution)/shard_map/while/body/eval_jaxpr/ppermute | solution.py:21
  158.5 14.7 %collective-permute-start = (bf16[256,512]{1,0:T(8,128)(2,1)S(1)}, bf16[256,512]{1,0:T(8,128)(2,1)S(1)}, u32[]{:S(2)}, u32[]{:S(2)}) collective-permute-start(bf16[256,512]{1,0:T(8,128)(2,1)S(1)} %bitcast.92), channel_id=1, source_target_pairs={{2,0},{4,2},{6,4},{8,6},{10,8},{12,10},{14,12},{16,14},{18,16},{20... | collective-permute-start | bytes 786440 | tf_op jit(solution)/shard_map/while/body/eval_jaxpr/ppermute | solution.py:23
  174.2 2.0 copy-start.3
  180.1 10.5 %collective-permute-start.1 = (bf16[256,512]{1,0:T(8,128)(2,1)S(1)}, bf16[256,512]{1,0:T(8,128)(2,1)S(1)}, u32[]{:S(2)}, u32[]{:S(2)}) collective-permute-start(bf16[256,512]{1,0:T(8,128)(2,1)S(1)} %bitcast.93), channel_id=1, source_target_pairs={{0,2},{2,4},{4,6},{6,8},{8,10},{10,12},{12,14},{14,16},{16,18},{18... | collective-permute-start | bytes 786440 | tf_op jit(solution)/shard_map/while/body/eval_jaxpr/ppermute | solution.py:21
  180.5 14.4 %collective-permute-start = (bf16[256,512]{1,0:T(8,128)(2,1)S(1)}, bf16[256,512]{1,0:T(8,128)(2,1)S(1)}, u32[]{:S(2)}, u32[]{:S(2)}) collective-permute-start(bf16[256,512]{1,0:T(8,128)(2,1)S(1)} %bitcast.92), channel_id=1, source_target_pairs={{2,0},{4,2},{6,4},{8,6},{10,8},{12,10},{14,12},{16,14},{18,16},{20... | collective-permute-start | bytes 786440 | tf_op jit(solution)/shard_map/while/body/eval_jaxpr/ppermute | solution.py:23
  195.9 2.0 copy-start.3
  201.8 11.7 %collective-permute-start.1 = (bf16[256,512]{1,0:T(8,128)(2,1)S(1)}, bf16[256,512]{1,0:T(8,128)(2,1)S(1)}, u32[]{:S(2)}, u32[]{:S(2)}) collective-permute-start(bf16[256,512]{1,0:T(8,128)(2,1)S(1)} %bitcast.93), channel_id=1, source_target_pairs={{0,2},{2,4},{4,6},{6,8},{8,10},{10,12},{12,14},{14,16},{16,18},{18... | collective-permute-start | bytes 786440 | tf_op jit(solution)/shard_map/while/body/eval_jaxpr/ppermute | solution.py:21
  202.2 11.7 %collective-permute-start = (bf16[256,512]{1,0:T(8,128)(2,1)S(1)}, bf16[256,512]{1,0:T(8,128)(2,1)S(1)}, u32[]{:S(2)}, u32[]{:S(2)}) collective-permute-start(bf16[256,512]{1,0:T(8,128)(2,1)S(1)} %bitcast.92), channel_id=1, source_target_pairs={{2,0},{4,2},{6,4},{8,6},{10,8},{12,10},{14,12},{16,14},{18,16},{20... | collective-permute-start | bytes 786440 | tf_op jit(solution)/shard_map/while/body/eval_jaxpr/ppermute | solution.py:23
  214.9 2.0 copy-start.3
  220.8 12.4 %collective-permute-start.1 = (bf16[256,512]{1,0:T(8,128)(2,1)S(1)}, bf16[256,512]{1,0:T(8,128)(2,1)S(1)}, u32[]{:S(2)}, u32[]{:S(2)}) collective-permute-start(bf16[256,512]{1,0:T(8,128)(2,1)S(1)} %bitcast.93), channel_id=1, source_target_pairs={{0,2},{2,4},{4,6},{6,8},{8,10},{10,12},{12,14},{14,16},{16,18},{18... | collective-permute-start | bytes 786440 | tf_op jit(solution)/shard_map/while/body/eval_jaxpr/ppermute | solution.py:21
  222.7 10.5 %collective-permute-start = (bf16[256,512]{1,0:T(8,128)(2,1)S(1)}, bf16[256,512]{1,0:T(8,128)(2,1)S(1)}, u32[]{:S(2)}, u32[]{:S(2)}) collective-permute-start(bf16[256,512]{1,0:T(8,128)(2,1)S(1)} %bitcast.92), channel_id=1, source_target_pairs={{2,0},{4,2},{6,4},{8,6},{10,8},{12,10},{14,12},{16,14},{18,16},{20... | collective-permute-start | bytes 786440 | tf_op jit(solution)/shard_map/while/body/eval_jaxpr/ppermute | solution.py:23
  234.3 2.0 copy-start.3
  240.2 11.9 %collective-permute-start.1 = (bf16[256,512]{1,0:T(8,128)(2,1)S(1)}, bf16[256,512]{1,0:T(8,128)(2,1)S(1)}, u32[]{:S(2)}, u32[]{:S(2)}) collective-permute-start(bf16[256,512]{1,0:T(8,128)(2,1)S(1)} %bitcast.93), channel_id=1, source_target_pairs={{0,2},{2,4},{4,6},{6,8},{8,10},{10,12},{12,14},{14,16},{16,18},{18... | collective-permute-start | bytes 786440 | tf_op jit(solution)/shard_map/while/body/eval_jaxpr/ppermute | solution.py:21
  242.5 11.8 %collective-permute-start = (bf16[256,512]{1,0:T(8,128)(2,1)S(1)}, bf16[256,512]{1,0:T(8,128)(2,1)S(1)}, u32[]{:S(2)}, u32[]{:S(2)}) collective-permute-start(bf16[256,512]{1,0:T(8,128)(2,1)S(1)} %bitcast.92), channel_id=1, source_target_pairs={{2,0},{4,2},{6,4},{8,6},{10,8},{12,10},{14,12},{16,14},{18,16},{20... | collective-permute-start | bytes 786440 | tf_op jit(solution)/shard_map/while/body/eval_jaxpr/ppermute | solution.py:23
  255.3 2.0 copy-start.3
  262.0 14.2 %copy-start.1 = (bf16[4,128,512]{2,1,0:T(8,128)(2,1)S(1)}, bf16[4,128,512]{2,1,0:T(8,128)(2,1)}, u32[]{:S(2)}) copy-start(bf16[4,128,512]{2,1,0:T(8,128)(2,1)} %copy-done) | copy-start | bytes 1572868
  262.0 119.3 %reduce-scatter.2.cloned.1.call-start = ((), (), s32[]{:S(2)}) async-start(), calls=%async_computation.2 | async-start | bytes 4456448 | tf_op jit(solution)/shard_map/reduce_scatter | solution.py:108
  263.1 5.4 %collective-permute-start.3 = (bf16[256,512]{1,0:T(8,128)(2,1)S(1)}, bf16[256,512]{1,0:T(8,128)(2,1)S(1)}, u32[]{:S(2)}, u32[]{:S(2)}) collective-permute-start(bf16[256,512]{1,0:T(8,128)(2,1)S(1)} %bitcast.96), channel_id=1, source_target_pairs={{2,0},{4,2},{6,4},{8,6},{10,8},{12,10},{14,12},{16,14},{18,16},{20... | collective-permute-start | bytes 786440 | tf_op jit(solution)/shard_map/ppermute | solution.py:23
  264.2 11.9 %collective-permute-start.2 = (bf16[256,512]{1,0:T(8,128)(2,1)S(1)}, bf16[256,512]{1,0:T(8,128)(2,1)S(1)}, u32[]{:S(2)}, u32[]{:S(2)}) collective-permute-start(bf16[256,512]{1,0:T(8,128)(2,1)S(1)} %bitcast.95), channel_id=1, source_target_pairs={{0,2},{2,4},{4,6},{6,8},{8,10},{10,12},{12,14},{14,16},{16,18},{18... | collective-permute-start | bytes 786440 | tf_op jit(solution)/shard_map/ppermute | solution.py:21
  277.2 2.0 copy-start.4
  280.7 2.1 copy-start.6
  (22 other events, 27.5 us)
Sparse Core Ops, SparseCore 0:
  262.1 9.2 all-gather.1
  286.1 95.1 reduce-scatter.1
where the time goes:
time: 393 us; the launch traced here: 390 us
  waiting for transfers between devices  143 us (36%)
  local copies, waits for them, and re-layouts  83.2 us (21%)
  starting transfers between devices  65 us (17%)
  matrix products  47.6 us (12%)
  other arithmetic  36.2 us (9%)
  between operations  14.2 us (4%)
    reduce_scatter x1, waiting for transfers between devices, shards(): lax.psum_scatter(jnp.stack([gram_part, projected_part], axis=1), 'atoms',...  95.3 us
    ppermute x13, starting transfers between devices, padded(): lax.ppermute(head, axis, [((i + 1) % count, i) for i in range(count)])  54 us
    ppermute x13, waiting for transfers between devices, padded(): lax.ppermute(head, axis, [((i + 1) % count, i) for i in range(count)])  33.6 us
    gather x13, local copies, waits for them, and re-layouts, hop_apply(): picked = window[local_index]  25.5 us
    dot_general x13, matrix products, hop_apply(): jnp.einsum('rji,rjc->ric', onsite_rows, own_rows, preferred_element_type=...  22.2 us
    while x96, local copies, waits for them, and re-layouts  20.3 us
    dot_general x13, matrix products, hop_apply(): jnp.einsum('rij,rjc->ric', onsite_rows, own_rows, preferred_element_type=...  16.4 us
    dynamic_slice x12, local copies, waits for them, and re-layouts, one_step(): scale_table[step_index] * (applied - center * current.astype(jnp.float32))  15.6 us
  transfers between devices with their start and end apart: 28, of which 18 were waited for; matrix products, arithmetic and copies ran while one was open for 19% of the time, Pallas kernels for 0%

commit v1 on v0

v1 whole, which is shorter than its diff:
```python
import functools

import jax
import jax.numpy as jnp
from jax import lax
from jax.experimental import pallas as pl
from jax.experimental.pallas import tpu as pltpu
from jax.sharding import PartitionSpec as P

DEG = 12
GROUP = 4
MESH = pl.DeviceIdType.MESH

filter_low = -0.5
filter_top = 4.0
filter_bottom = -1.6


def filter_coefficients(degree):
    center = 0.5 * (filter_top + filter_low)
    half_width = 0.5 * (filter_top - filter_low)
    sigma_first = half_width / (filter_bottom - center)
    listed = [(sigma_first / half_width, 0.0)]
    sigma_now = sigma_first
    for degree_step in range(1, degree):
        sigma_next = 1.0 / (2.0 / sigma_first - sigma_now)
        listed.append((2.0 * sigma_next / half_width, sigma_now * sigma_next))
        sigma_now = sigma_next
    return center, listed


def at_rows(start, size):
    return pl.ds(pl.multiple_of(start, size), size)


def kernel(
    dims,
    coef,
    start,
    hown,
    filtered,
    gram,
    projected,
    hbuf,
    y,
    fall,
    xt,
    part,
    inbox,
    local_sem,
    h_send,
    h_recv,
    hf_send,
    hf_recv,
    v_send,
    v_recv,
    halo_send,
    halo_recv,
    f_send,
    f_recv,
    ff_send,
    ff_recv,
    p_send,
    p_recv,
):
    count, blk, own_blocks = dims["count"], dims["blk"], dims["own_blocks"]
    group = GROUP
    slabs = count // group
    rows_dev = own_blocks * blk
    rows_slab = group * rows_dev
    wide = start.shape[1] // group
    pairs_dev = own_blocks // 2
    pairs = pairs_dev * group
    two = 2 * blk
    six = 6 * blk
    piece = gram.shape[0]
    me = lax.axis_index("atoms")
    core = lax.axis_index("vecs")
    other = 1 - core
    p = lax.rem(me, group)
    slab = lax.div(me, group)
    base = slab * group
    right = lax.rem(slab + 1, slabs) * group + p
    left = lax.rem(slab + slabs - 1, slabs) * group + p

    barrier = pltpu.get_barrier_semaphore()

    def greet(step, carry):
        peer = lax.rem(me + step, count)
        pl.semaphore_signal(
            barrier, inc=1, device_id={"atoms": peer, "vecs": core}, device_id_type=MESH
        )
        return carry

    lax.fori_loop(1, count, greet, 0)
    pl.semaphore_signal(barrier, inc=1, device_id={"atoms": me, "vecs": other}, device_id_type=MESH)

    own_h = pltpu.make_async_copy(
        hown, hbuf.at[pl.ds(p * pairs_dev, pairs_dev)], local_sem.at[0]
    )
    own_h.start()
    own_v = pltpu.make_async_copy(
        start.at[:, at_rows(p * wide, wide)],
        y.at[0, at_rows(two + p * rows_dev, two)]
        if rows_dev == two
        else y.at[0, pl.ds(pl.multiple_of(two + p * rows_dev, two), rows_dev)],
        local_sem.at[1],
    )
    own_v.start()
    y[1, two : two + rows_slab, :] = jnp.zeros((rows_slab, wide), jnp.bfloat16)

    pl.semaphore_wait(barrier, count)

    def peer_id(index, which):
        return {"atoms": index, "vecs": which}

    half = pairs_dev // 2

    def h_copy(source, target, step):
        return pltpu.make_async_remote_copy(
            src_ref=hown.at[pl.ds(core * half, half)],
            dst_ref=hbuf.at[pl.ds(source * pairs_dev + core * half, half)],
            send_sem=h_send.at[step],
            recv_sem=h_recv.at[step],
            device_id=peer_id(base + target, core),
            device_id_type=MESH,
        )

    def h_forward(source, step, which):
        where = pl.ds(source * pairs_dev + which * half, half)
        return pltpu.make_async_remote_copy(
            src_ref=hbuf.at[where],
            dst_ref=hbuf.at[where],
            send_sem=hf_send.at[step],
            recv_sem=hf_recv.at[step],
            device_id=peer_id(me, other),
            device_id_type=MESH,
        )

    def v_copy(source, target, step):
        return pltpu.make_async_remote_copy(
            src_ref=start.at[:, at_rows(target * wide, wide)],
            dst_ref=y.at[0, pl.ds(pl.multiple_of(two + source * rows_dev, two), rows_dev)],
            send_sem=v_send.at[step],
            recv_sem=v_recv.at[step],
            device_id=peer_id(base + target, core),
            device_id_type=MESH,
        )

    to = [lax.rem(p + step, group) for step in range(group)]
    source_of = [lax.rem(p + group - step, group) for step in range(group)]
    steps = (3, 1, 2)
    for step in steps:
        h_copy(p, to[step], step).start()
    for step in steps:
        v_copy(p, to[step], step).start()
    own_v.wait()
    own_h.wait()
    for step in steps:
        h_copy(source_of[step], p, step).wait_recv()
        h_forward(source_of[step], step, core).start()
    for step in steps:
        v_copy(source_of[step], p, step).wait_recv()

    def halo(slot, side):
        low = slice(two, 2 * two)
        high = slice(rows_slab, rows_slab + two)
        src = (high, low)[side]
        dst = (slice(0, two), slice(rows_slab + two, rows_slab + 2 * two))[side]
        return pltpu.make_async_remote_copy(
            src_ref=y.at[slot, src],
            dst_ref=y.at[slot, dst],
            send_sem=halo_send.at[slot, side],
            recv_sem=halo_recv.at[slot, side],
            device_id=peer_id((right, left)[side], core),
            device_id_type=MESH,
        )

    for side in (0, 1):
        halo(0, side).start()
    for step in steps:
        h_forward(source_of[step], step, other).wait_recv()

    def one_pair(src, dst, index, scale, shift, carry):
        window = y[src, pl.ds(pl.multiple_of(index * two, two), six), :]
        total = jnp.dot(hbuf[index], window, preferred_element_type=jnp.float32)
        mine = pl.ds(pl.multiple_of(index * two + two, two), two)
        now = y[src, mine, :].astype(jnp.float32)
        before = y[dst, mine, :].astype(jnp.float32)
        y[dst, mine, :] = (scale * total - shift * now - carry * before).astype(jnp.bfloat16)

    def one_step(step, last):
        dst = lax.rem(step, 2)
        src = 1 - dst
        scale, shift, carry = coef[3 * step], coef[3 * step + 1], coef[3 * step + 2]
        for side in (0, 1):
            halo(src, side).wait_recv()
        one_pair(src, dst, 0, scale, shift, carry)
        one_pair(src, dst, pairs - 1, scale, shift, carry)
        if not last:
            for side in (0, 1):
                halo(dst, side).start()
        for index in range(1, pairs - 1):
            one_pair(src, dst, index, scale, shift, carry)
        for side in (0, 1):
            halo(src, side).wait_send()

    def looped(step, state):
        one_step(step, False)
        return state

    lax.fori_loop(1, DEG + 1, looped, 0)
    final_slot = DEG % 2
    own = slice(two, two + rows_slab)

    def f_copy(source, target, step):
        return pltpu.make_async_remote_copy(
            src_ref=y.at[final_slot, own],
            dst_ref=fall.at[source, core],
            send_sem=f_send.at[step],
            recv_sem=f_recv.at[step],
            device_id=peer_id(base + target, core),
            device_id_type=MESH,
        )

    def f_forward(source, step, which):
        return pltpu.make_async_remote_copy(
            src_ref=y.at[final_slot, own] if step == 0 else fall.at[source, which],
            dst_ref=fall.at[source, which],
            send_sem=ff_send.at[step],
            recv_sem=ff_recv.at[step],
            device_id=peer_id(me, other),
            device_id_type=MESH,
        )

    for step in steps:
        f_copy(p, to[step], step).start()
    f_forward(p, 0, core).start()
    own_f = pltpu.make_async_copy(y.at[final_slot, own], fall.at[p, core], local_sem.at[2])
    own_f.start()
    one_step(DEG + 1, True)
    xt[0:wide, :] = y[final_slot, own, :].T
    xt[wide : 2 * wide, :] = y[1 - final_slot, own, :].T
    own_f.wait()

    owners = wide // piece

    def p_copy(owner, slot_from):
        return pltpu.make_async_remote_copy(
            src_ref=part.at[owner],
            dst_ref=inbox.at[slot_from],
            send_sem=p_send.at[owner],
            recv_sem=p_recv.at[slot_from],
            device_id=peer_id(owner, core),
            device_id_type=MESH,
        )

    def p_local():
        return pltpu.make_async_copy(part.at[me], inbox.at[me], p_recv.at[me])

    def strip(source, which):
        block = jnp.dot(xt[...], fall[source, which], preferred_element_type=jnp.float32)
        turned = block.T.reshape(owners, piece, 2 * wide).astype(jnp.bfloat16)
        first = (which * group + source) * owners
        part[pl.ds(first, owners)] = turned

        def send(index, state):
            owner = first + index

            @pl.when(owner != me)
            def _():
                p_copy(owner, me).start()

            @pl.when(owner == me)
            def _():
                p_local().start()

            return state

        lax.fori_loop(0, owners, send, 0)

    strip(p, core)
    f_forward(p, 0, other).wait_recv()
    strip(p, other)
    for step in steps:
        f_copy(source_of[step], p, step).wait_recv()
        f_forward(source_of[step], step, core).start()
        strip(source_of[step], core)
        f_forward(source_of[step], step, other).wait_recv()
        strip(source_of[step], other)
    for source in range(group):
        filtered[:, source * wide : (source + 1) * wide] = fall[
            source, core, pl.ds(pl.multiple_of(p * rows_dev, two), rows_dev), :
        ]

    def arrive(index, state):
        @pl.when(index != me)
        def _():
            p_copy(me, index).wait_recv()

        @pl.when(index == me)
        def _():
            p_local().wait()

        return state

    lax.fori_loop(0, count, arrive, 0)
    unit = 1.0 / (slabs * rows_slab)
    for source in range(group):

        def add(index, total):
            return total + inbox[index * group + source].astype(jnp.float32)

        summed = lax.fori_loop(0, slabs, add, jnp.zeros((piece, 2 * wide), jnp.float32)) * unit
        gram[:, source * wide : (source + 1) * wide] = summed[:, :wide]
        projected[:, source * wide : (source + 1) * wide] = summed[:, wide:]

    for step in steps:
        h_copy(p, to[step], step).wait_send()
        h_forward(source_of[step], step, core).wait_send()
        v_copy(p, to[step], step).wait_send()
        f_copy(p, to[step], step).wait_send()
        f_forward(source_of[step], step, core).wait_send()
    f_forward(p, 0, core).wait_send()

    def left_out(index, state):
        @pl.when(index != me)
        def _():
            p_copy(index, me).wait_send()

        return state

    lax.fori_loop(0, count, left_out, 0)


def shards(start_block, onsite, hopping, columns, counts):
    own_blocks, blk = onsite.shape[0], onsite.shape[1]
    slots = columns.shape[1]
    reach = slots // 2
    span = 2 * reach + 1
    count = lax.axis_size("atoms")
    cores = lax.axis_size("vecs")
    total_blocks = own_blocks * count
    width = start_block.shape[1]
    wide = width // GROUP
    piece = width * cores // count
    slabs = count // GROUP
    rows_slab = GROUP * own_blocks * blk
    pairs_dev = own_blocks // 2

    center, listed = filter_coefficients(DEG)
    coef = [(0.0, 0.0, 0.0)]
    coef += [(scale, scale * center, carry) for scale, carry in listed]
    coef += [(1.0, 0.0, 0.0)]
    table = jnp.array(coef, jnp.float32).reshape(-1)

    first = lax.axis_index("atoms") * own_blocks
    row_ids = first + jnp.arange(own_blocks, dtype=jnp.int32)
    offset = jnp.mod(columns - row_ids[:, None] + reach, total_blocks)
    live = jnp.arange(slots, dtype=jnp.int32)[None, :] < counts[:, None]
    wide_onsite = onsite.astype(jnp.float32)
    direct = (0.5 * (wide_onsite + jnp.swapaxes(wide_onsite, 1, 2))).astype(jnp.bfloat16)
    zero = jnp.zeros((), jnp.bfloat16)
    zeros = jnp.zeros((blk, blk), jnp.bfloat16)
    pair_rows = []
    for row in range(own_blocks):
        line = []
        for shift in range(span):
            block = direct[row] if shift == reach else zeros
            for slot in range(slots):
                chosen = live[row, slot] & (offset[row, slot] == shift)
                block = jnp.where(chosen, hopping[row, slot], block)
            line.append(block)
        line = line + [zeros] if row % 2 == 0 else [zeros] + line
        pair_rows.append(jnp.concatenate(line, axis=1))
    hown = jnp.concatenate(pair_rows, axis=0).reshape(pairs_dev, 2 * blk, 6 * blk)

    dims = {"count": count, "blk": blk, "own_blocks": own_blocks}
    vmem = pl.BlockSpec(memory_space=pltpu.VMEM)
    dma = pltpu.SemaphoreType.DMA
    return pl.pallas_call(
        functools.partial(kernel, dims),
        out_shape=(
            jax.ShapeDtypeStruct(start_block.shape, jnp.bfloat16),
            jax.ShapeDtypeStruct((piece, width), jnp.float32),
            jax.ShapeDtypeStruct((piece, width), jnp.float32),
        ),
        in_specs=[pl.BlockSpec(memory_space=pltpu.SMEM), vmem, vmem],
        out_specs=(vmem, vmem, vmem),
        scratch_shapes=[
            pltpu.VMEM((pairs_dev * GROUP, 2 * blk, 6 * blk), jnp.bfloat16),
            pltpu.VMEM((2, rows_slab + 4 * blk, wide), jnp.bfloat16),
            pltpu.VMEM((GROUP, cores, rows_slab, wide), jnp.bfloat16),
            pltpu.VMEM((2 * wide, rows_slab), jnp.bfloat16),
            pltpu.VMEM((count, piece, 2 * wide), jnp.bfloat16),
            pltpu.VMEM((count, piece, 2 * wide), jnp.bfloat16),
            dma((3,)),
            dma((GROUP,)),
            dma((GROUP,)),
            dma((GROUP,)),
            dma((GROUP,)),
            dma((GROUP,)),
            dma((GROUP,)),
            dma((2, 2)),
            dma((2, 2)),
            dma((GROUP,)),
            dma((GROUP,)),
            dma((GROUP,)),
            dma((GROUP,)),
            dma((count,)),
            dma((count,)),
        ],
        compiler_params=pltpu.CompilerParams(
            collective_id=0, has_side_effects=True, vmem_limit_bytes=48 * 1024 * 1024
        ),
    )(table, start_block, hown)


def solution(mesh):
    in_specs = (
        P("atoms", "vecs"),
        P("atoms", None, None),
        P("atoms", None, None, None),
        P("atoms", None),
        P("atoms"),
    )
    out_specs = (P("atoms", "vecs"), P("atoms", "vecs"), P("atoms", "vecs"))
    return jax.shard_map(shards, mesh=mesh, in_specs=in_specs, out_specs=out_specs, check_vma=False)
```

time: 393 us -> 235 us (0.60)
  waiting for transfers between devices: 143 us -> 0 us
  Pallas kernels: 0 us -> 123 us
  between operations: 14.2 us -> 102 us
  local copies, waits for them, and re-layouts: 83.2 us -> 5.66 us
  starting transfers between devices: 65 us -> 0 us
  matrix products: 47.6 us -> 0 us
  other arithmetic: 36.2 us -> 2.36 us
    pallas_call x0 -> x1, Pallas kernels: none -> 123 us  [shards(): pl.pallas_call(functools.partial(kernel, dims), out_shape=(jax.ShapeDtype...]
    reduce_scatter x1 -> x0, waiting for transfers between devices: 95.3 us -> none  [shards(): lax.psum_scatter(jnp.stack([gram_part, projected_part], axis=1), 'atoms',...]
    ppermute x26 -> x0, starting transfers between devices: 64.9 us -> none  [the longest x13 54 us: padded(): lax.ppermute(head, axis, [((i + 1) % count, i) for i in range(count)])]
    dot_general x41 -> x0, matrix products: 47.6 us -> none  [the longest x13 22.2 us: hop_apply(): jnp.einsum('rji,rjc->ric', onsite_rows, own_rows, preferred_element_type=...]
    ppermute x26 -> x0, waiting for transfers between devices: 47.3 us -> none  [the longest x13 33.6 us: padded(): lax.ppermute(head, axis, [((i + 1) % count, i) for i in range(count)])]
    dynamic_slice x24 -> x0, local copies, waits for them, and re-layouts: 30.3 us -> none  [the longest x12 15.6 us: one_step(): scale_table[step_index] * (applied - center * current.astype(jnp.float32))]
    gather x13 -> x0, local copies, waits for them, and re-layouts: 25.5 us -> none  [hop_apply(): picked = window[local_index]]
    while x96 -> x0, local copies, waits for them, and re-layouts: 20.3 us -> none
  transfers between devices with their start and end apart: 28 -> 0, of which waited for: 18 -> 0; matrix products, arithmetic and copies ran while one was open for 19% -> 0% of each run, Pallas kernels for 0% -> 0%
where the time goes in v1:
time: 235 us; the launch traced here: 233 us
  Pallas kernels  123 us (52%)
  between operations  102 us (43%)
  local copies, waits for them, and re-layouts  5.66 us (2%)
  other arithmetic  2.36 us (1%)
    pallas_call x1, Pallas kernels, shards(): pl.pallas_call(functools.partial(kernel, dims), out_shape=(jax.ShapeDtype...  123 us

profile of v1, /device:TPU:1, one launch (start us, length us, event | category | flops | bytes accessed | tf_op | source)
XLA Modules:
  0.0 233.4 jit_solution(9166618662278391372)
XLA Ops:
  0.6 0.0 copy-start.2
  0.7 0.8 iota_compare_fusion
  1.4 0.8 add_select_fusion
  2.2 0.7 fusion.67
  53.3 0.7 fusion.68
  105.1 1.0 copy.9
  106.1 0.0 copy-done.2
  106.2 0.1 constant_dynamic-update-slice_fusion.5
  106.2 0.1 constant_dynamic-update-slice_fusion.4
  106.3 0.1 copy.10
  106.5 0.1 constant_dynamic-update-slice_fusion.3
  106.5 0.1 constant_dynamic-update-slice_fusion.2
  106.6 0.1 constant_dynamic-update-slice_fusion.1
  106.8 0.1 constant_dynamic-update-slice_fusion.8
  106.8 0.1 constant_dynamic-update-slice_fusion.7
  106.9 0.1 constant_dynamic-update-slice_fusion.6
  107.0 0.0 copy-start
  107.1 0.0 copy-start.1
  107.1 0.1 pad_maximum_fusion
  107.1 1.0 copy-done
  108.1 0.0 copy-done.1
  108.1 123.2 %shard_map.85 = (bf16[512,512]{1,0:T(8,128)(2,1)S(1)}, f32[64,512]{1,0:T(8,128)S(1)}, f32[64,512]{1,0:T(8,128)S(1)}) custom-call(f32[42]{0:T(128)S(1)} %copy-done.1, bf16[512,512]{1,0:T(8,128)(2,1)S(1)} %copy-done, bf16[2,256,768]{2,1,0:T(8,128)(2,1)S(1)} %bitcast.359), custom_call_target="tpu_custom_call" | custom-call | tf_op jit(solution)/shard_map/pallas_call | solution.py:381
  231.3 0.8 copy.34
  232.1 0.7 copy.35
  232.7 0.7 copy.36
  (9 shorter events, 0.2 us)
Async XLA Ops:
  0.6 105.5 %copy-start.2 = (bf16[4,4,128,128]{3,2,1,0:T(8,128)(2,1)S(1)}, bf16[4,4,128,128]{3,2,1,0:T(8,128)(2,1)}, u32[]{:S(2)}) copy-start(bf16[4,4,128,128]{3,2,1,0:T(8,128)(2,1)} %param.8) | copy-start | bytes 1572868
  107.0 1.0 copy-start
  107.1 1.0 copy-start.1

commit v2 on v1

--- a/solution.py
+++ b/solution.py
@@ -36,11 +36,15 @@
 def kernel(
     dims,
     coef,
+    columns,
+    counts,
     start,
-    hown,
+    onsite,
+    hopping,
     filtered,
     gram,
     projected,
+    hown,
     hbuf,
     y,
     fall,
@@ -66,6 +70,7 @@
     count, blk, own_blocks = dims["count"], dims["blk"], dims["own_blocks"]
     group = GROUP
     slabs = count // group
+    total_blocks = own_blocks * count
     rows_dev = own_blocks * blk
     rows_slab = group * rows_dev
     wide = start.shape[1] // group
@@ -95,19 +100,38 @@
     lax.fori_loop(1, count, greet, 0)
     pl.semaphore_signal(barrier, inc=1, device_id={"atoms": me, "vecs": other}, device_id_type=MESH)
 
-    own_h = pltpu.make_async_copy(
-        hown, hbuf.at[pl.ds(p * pairs_dev, pairs_dev)], local_sem.at[0]
-    )
-    own_h.start()
     own_v = pltpu.make_async_copy(
         start.at[:, at_rows(p * wide, wide)],
         y.at[0, at_rows(two + p * rows_dev, two)]
         if rows_dev == two
         else y.at[0, pl.ds(pl.multiple_of(two + p * rows_dev, two), rows_dev)],
-        local_sem.at[1],
+        local_sem.at[0],
     )
     own_v.start()
     y[1, two : two + rows_slab, :] = jnp.zeros((rows_slab, wide), jnp.bfloat16)
+
+    slots, reach = hopping.shape[1], dims["reach"]
+    zeros = jnp.zeros((blk, blk), jnp.bfloat16)
+    for row in range(own_blocks):
+        pair, half_row = row // 2, row % 2
+        lines = slice(half_row * blk, (half_row + 1) * blk)
+        offsets = []
+        for slot in range(slots):
+            ahead = columns[row, slot] - (me * own_blocks + row) + reach + total_blocks
+            offset = lax.rem(ahead, total_blocks)
+            offsets.append(jnp.where(slot < counts[row], offset, -1))
+        for shift in range(2 * reach + 1):
+            if shift == reach:
+                wide_block = onsite[row].astype(jnp.float32)
+                block = (0.5 * (wide_block + wide_block.T)).astype(jnp.bfloat16)
+            else:
+                block = zeros
+                for slot in range(slots):
+                    block = jnp.where(offsets[slot] == shift, hopping[row, slot], block)
+            place = half_row + shift
+            hown[pair, lines, place * blk : (place + 1) * blk] = block
+        empty = (1 - half_row) * 5
+        hown[pair, lines, empty * blk : (empty + 1) * blk] = zeros
 
     pl.semaphore_wait(barrier, count)
 
@@ -154,8 +178,8 @@
         h_copy(p, to[step], step).start()
     for step in steps:
         v_copy(p, to[step], step).start()
+    hbuf[pl.ds(p * pairs_dev, pairs_dev)] = hown[...]
     own_v.wait()
-    own_h.wait()
     for step in steps:
         h_copy(source_of[step], p, step).wait_recv()
         h_forward(source_of[step], step, core).start()
@@ -236,7 +260,7 @@
     for step in steps:
         f_copy(p, to[step], step).start()
     f_forward(p, 0, core).start()
-    own_f = pltpu.make_async_copy(y.at[final_slot, own], fall.at[p, core], local_sem.at[2])
+    own_f = pltpu.make_async_copy(y.at[final_slot, own], fall.at[p, core], local_sem.at[1])
     own_f.start()
     one_step(DEG + 1, True)
     xt[0:wide, :] = y[final_slot, own, :].T
@@ -335,12 +359,8 @@
 
 def shards(start_block, onsite, hopping, columns, counts):
     own_blocks, blk = onsite.shape[0], onsite.shape[1]
-    slots = columns.shape[1]
-    reach = slots // 2
-    span = 2 * reach + 1
     count = lax.axis_size("atoms")
     cores = lax.axis_size("vecs")
-    total_blocks = own_blocks * count
     width = start_block.shape[1]
     wide = width // GROUP
     piece = width * cores // count
@@ -354,29 +374,9 @@
     coef += [(1.0, 0.0, 0.0)]
     table = jnp.array(coef, jnp.float32).reshape(-1)
 
-    first = lax.axis_index("atoms") * own_blocks
-    row_ids = first + jnp.arange(own_blocks, dtype=jnp.int32)
-    offset = jnp.mod(columns - row_ids[:, None] + reach, total_blocks)
-    live = jnp.arange(slots, dtype=jnp.int32)[None, :] < counts[:, None]
-    wide_onsite = onsite.astype(jnp.float32)
-    direct = (0.5 * (wide_onsite + jnp.swapaxes(wide_onsite, 1, 2))).astype(jnp.bfloat16)
-    zero = jnp.zeros((), jnp.bfloat16)
-    zeros = jnp.zeros((blk, blk), jnp.bfloat16)
-    pair_rows = []
-    for row in range(own_blocks):
-        line = []
-        for shift in range(span):
-            block = direct[row] if shift == reach else zeros
-            for slot in range(slots):
-                chosen = live[row, slot] & (offset[row, slot] == shift)
-                block = jnp.where(chosen, hopping[row, slot], block)
-            line.append(block)
-        line = line + [zeros] if row % 2 == 0 else [zeros] + line
-        pair_rows.append(jnp.concatenate(line, axis=1))
-    hown = jnp.concatenate(pair_rows, axis=0).reshape(pairs_dev, 2 * blk, 6 * blk)
-
-    dims = {"count": count, "blk": blk, "own_blocks": own_blocks}
+    dims = {"count": count, "blk": blk, "own_blocks": own_blocks, "reach": columns.shape[1] // 2}
     vmem = pl.BlockSpec(memory_space=pltpu.VMEM)
+    smem = pl.BlockSpec(memory_space=pltpu.SMEM)
     dma = pltpu.SemaphoreType.DMA
     return pl.pallas_call(
         functools.partial(kernel, dims),
@@ -385,16 +385,17 @@
             jax.ShapeDtypeStruct((piece, width), jnp.float32),
             jax.ShapeDtypeStruct((piece, width), jnp.float32),
         ),
-        in_specs=[pl.BlockSpec(memory_space=pltpu.SMEM), vmem, vmem],
+        in_specs=[smem, smem, smem, vmem, vmem, vmem],
         out_specs=(vmem, vmem, vmem),
         scratch_shapes=[
+            pltpu.VMEM((pairs_dev, 2 * blk, 6 * blk), jnp.bfloat16),
             pltpu.VMEM((pairs_dev * GROUP, 2 * blk, 6 * blk), jnp.bfloat16),
             pltpu.VMEM((2, rows_slab + 4 * blk, wide), jnp.bfloat16),
             pltpu.VMEM((GROUP, cores, rows_slab, wide), jnp.bfloat16),
             pltpu.VMEM((2 * wide, rows_slab), jnp.bfloat16),
             pltpu.VMEM((count, piece, 2 * wide), jnp.bfloat16),
             pltpu.VMEM((count, piece, 2 * wide), jnp.bfloat16),
-            dma((3,)),
+            dma((2,)),
             dma((GROUP,)),
             dma((GROUP,)),
             dma((GROUP,)),
@@ -413,7 +414,7 @@
         compiler_params=pltpu.CompilerParams(
             collective_id=0, has_side_effects=True, vmem_limit_bytes=48 * 1024 * 1024
         ),
-    )(table, start_block, hown)
+    )(table, columns, counts, start_block, onsite, hopping)
 
 
 def solution(mesh):

time: 235 us -> 131 us (0.56)
  between operations: 102 us -> 0.65 us
  other arithmetic: 2.36 us -> 0 us
    unnamed x12 -> x15, local copies, waits for them, and re-layouts: 4.12 us -> 7.08 us
where the time goes in v2:
time: 131 us
  Pallas kernels  123 us (94%)
  local copies, waits for them, and re-layouts  7.08 us (5%)
    pallas_call x1, Pallas kernels, shards(): pl.pallas_call(functools.partial(kernel, dims), out_shape=(jax.ShapeDtype...  123 us
    unnamed x15, local copies, waits for them, and re-layouts  7.08 us

profile of v2, /device:TPU:1, one launch (start us, length us, event | category | flops | bytes accessed | tf_op | source)
XLA Modules:
  0.0 130.9 jit_solution(16590759615735228231)
XLA Ops:
  0.6 0.0 copy-start
  0.6 1.0 copy-done
  1.7 0.0 copy-start.1
  1.7 1.0 copy-done.1
  2.7 0.0 copy-start.2
  2.7 0.9 copy-done.2
  3.6 0.0 copy-start.3
  3.6 0.7 copy-done.3
  4.3 0.0 copy-start.4
  4.3 0.7 copy-done.4
  5.0 0.0 copy-start.5
  5.0 0.7 copy-done.5
  5.6 123.1 %shard_map.85 = (bf16[512,512]{1,0:T(8,128)(2,1)S(1)}, f32[64,512]{1,0:T(8,128)S(1)}, f32[64,512]{1,0:T(8,128)S(1)}) custom-call(f32[42]{0:T(128)S(1)} %copy-done.5, s32[4,4]{1,0:T(4,128)S(1)} %copy-done.3, s32[4]{0:T(128)S(1)} %copy-done.4, bf16[512,512]{1,0:T(8,128)(2,1)S(1)} %copy-done, bf16[4,128,128]{2,1,0:T(8,128)(2,1)S(1)} %copy-done.2, ...), custom_call_target="tpu_custom_call" | custom-call | tf_op jit(solution)/shard_map/pallas_call | solution.py:381
  128.8 0.8 copy.12
  129.6 0.7 copy.13
  130.2 0.7 copy.14
Async XLA Ops:
  0.6 1.0 copy-start
  1.7 1.0 copy-start.1
  2.7 0.9 copy-start.2
  3.6 0.7 copy-start.3
  4.3 0.7 copy-start.4
  5.0 0.7 copy-start.5

commit v3 on v2

--- a/solution.py
+++ b/solution.py
@@ -44,7 +44,6 @@
     filtered,
     gram,
     projected,
-    hown,
     hbuf,
     y,
     fall,
@@ -129,34 +128,41 @@
                 for slot in range(slots):
                     block = jnp.where(offsets[slot] == shift, hopping[row, slot], block)
             place = half_row + shift
-            hown[pair, lines, place * blk : (place + 1) * blk] = block
-        empty = (1 - half_row) * 5
-        hown[pair, lines, empty * blk : (empty + 1) * blk] = zeros
+            hbuf[p * pairs_dev + pair, lines, place * blk : (place + 1) * blk] = block
+    for pair in range(pairs):
+        hbuf[pair, 0:blk, 5 * blk : six] = zeros
+        hbuf[pair, blk:two, 0:blk] = zeros
 
     pl.semaphore_wait(barrier, count)
 
     def peer_id(index, which):
         return {"atoms": index, "vecs": which}
 
-    half = pairs_dev // 2
-
-    def h_copy(source, target, step):
-        return pltpu.make_async_remote_copy(
-            src_ref=hown.at[pl.ds(core * half, half)],
-            dst_ref=hbuf.at[pl.ds(source * pairs_dev + core * half, half)],
-            send_sem=h_send.at[step],
-            recv_sem=h_recv.at[step],
-            device_id=peer_id(base + target, core),
-            device_id_type=MESH,
-        )
-
-    def h_forward(source, step, which):
-        where = pl.ds(source * pairs_dev + which * half, half)
-        return pltpu.make_async_remote_copy(
-            src_ref=hbuf.at[where],
-            dst_ref=hbuf.at[where],
-            send_sem=hf_send.at[step],
-            recv_sem=hf_recv.at[step],
+    side_of = (p, p + 1 - 2 * lax.rem(p, 2), lax.rem(p + 2, group), group - 1 - p)
+    steps = (1, 2, 3)
+    relays = ((1, 2), (2, 1))
+
+    def h_place(pair, row):
+        return (pair, slice(row * blk, (row + 1) * blk), slice(row * blk, (row + 5) * blk))
+
+    def h_copy(source, via, step, row):
+        place = h_place(source * pairs_dev + core, row)
+        return pltpu.make_async_remote_copy(
+            src_ref=hbuf.at[place],
+            dst_ref=hbuf.at[place],
+            send_sem=h_send.at[step, row],
+            recv_sem=h_recv.at[step, row],
+            device_id=peer_id(base + side_of[via], core),
+            device_id_type=MESH,
+        )
+
+    def h_forward(step, which, row):
+        place = h_place(side_of[step] * pairs_dev + which, row)
+        return pltpu.make_async_remote_copy(
+            src_ref=hbuf.at[place],
+            dst_ref=hbuf.at[place],
+            send_sem=hf_send.at[step, row],
+            recv_sem=hf_recv.at[step, row],
             device_id=peer_id(me, other),
             device_id_type=MESH,
         )
@@ -171,20 +177,25 @@
             device_id_type=MESH,
         )
 
-    to = [lax.rem(p + step, group) for step in range(group)]
-    source_of = [lax.rem(p + group - step, group) for step in range(group)]
-    steps = (3, 1, 2)
+    for row in (0, 1):
+        h_copy(p, 1 + row, 1 + row, row).start()
+    for row in (0, 1):
+        h_copy(p, 2 - row, 2 - row, row).start()
+    for row, (step, via) in enumerate(relays):
+        h_copy(side_of[step], step, step, row).wait_recv()
+        h_copy(side_of[step], via, 3, row).start()
+        h_forward(step, core, row).start()
     for step in steps:
-        h_copy(p, to[step], step).start()
+        v_copy(p, side_of[step], step).start()
+    own_v.wait()
+    for row, (step, via) in enumerate(relays):
+        h_copy(side_of[via], via, via, row).wait_recv()
+        h_forward(via, core, row).start()
+    for row in (0, 1):
+        h_copy(side_of[3], 3, 3, row).wait_recv()
+        h_forward(3, core, row).start()
     for step in steps:
-        v_copy(p, to[step], step).start()
-    hbuf[pl.ds(p * pairs_dev, pairs_dev)] = hown[...]
-    own_v.wait()
-    for step in steps:
-        h_copy(source_of[step], p, step).wait_recv()
-        h_forward(source_of[step], step, core).start()
-    for step in steps:
-        v_copy(source_of[step], p, step).wait_recv()
+        v_copy(side_of[step], p, step).wait_recv()
 
     def halo(slot, side):
         low = slice(two, 2 * two)
@@ -203,7 +214,8 @@
     for side in (0, 1):
         halo(0, side).start()
     for step in steps:
-        h_forward(source_of[step], step, other).wait_recv()
+        for row in (0, 1):
+            h_forward(step, other, row).wait_recv()
 
     def one_pair(src, dst, index, scale, shift, carry):
         window = y[src, pl.ds(pl.multiple_of(index * two, two), six), :]
@@ -217,13 +229,11 @@
         dst = lax.rem(step, 2)
         src = 1 - dst
         scale, shift, carry = coef[3 * step], coef[3 * step + 1], coef[3 * step + 2]
-        for side in (0, 1):
+        for side, edge in ((0, 0), (1, pairs - 1)):
             halo(src, side).wait_recv()
-        one_pair(src, dst, 0, scale, shift, carry)
-        one_pair(src, dst, pairs - 1, scale, shift, carry)
-        if not last:
-            for side in (0, 1):
-                halo(dst, side).start()
+            one_pair(src, dst, edge, scale, shift, carry)
+            if not last:
+                halo(dst, 1 - side).start()
         for index in range(1, pairs - 1):
             one_pair(src, dst, index, scale, shift, carry)
         for side in (0, 1):
@@ -237,29 +247,40 @@
     final_slot = DEG % 2
     own = slice(two, two + rows_slab)
 
-    def f_copy(source, target, step):
-        return pltpu.make_async_remote_copy(
-            src_ref=y.at[final_slot, own],
-            dst_ref=fall.at[source, core],
-            send_sem=f_send.at[step],
-            recv_sem=f_recv.at[step],
-            device_id=peer_id(base + target, core),
-            device_id_type=MESH,
-        )
-
-    def f_forward(source, step, which):
-        return pltpu.make_async_remote_copy(
-            src_ref=y.at[final_slot, own] if step == 0 else fall.at[source, which],
-            dst_ref=fall.at[source, which],
-            send_sem=ff_send.at[step],
-            recv_sem=ff_recv.at[step],
+    half = rows_slab // 2
+
+    def f_copy(source, via, step, part_of):
+        rows = slice(part_of * half, (part_of + 1) * half)
+        place = fall.at[source, core, rows]
+        own_rows = slice(two + part_of * half, two + (part_of + 1) * half)
+        return pltpu.make_async_remote_copy(
+            src_ref=place if step == 3 else y.at[final_slot, own_rows],
+            dst_ref=place,
+            send_sem=f_send.at[step, part_of],
+            recv_sem=f_recv.at[step, part_of],
+            device_id=peer_id(base + side_of[via], core),
+            device_id_type=MESH,
+        )
+
+    def f_forward(step, which, part_of):
+        rows = slice(part_of * half, (part_of + 1) * half)
+        own_rows = slice(two + part_of * half, two + (part_of + 1) * half)
+        place = fall.at[side_of[step], which, rows]
+        return pltpu.make_async_remote_copy(
+            src_ref=y.at[final_slot, own_rows] if step == 0 else place,
+            dst_ref=place,
+            send_sem=ff_send.at[step, part_of],
+            recv_sem=ff_recv.at[step, part_of],
             device_id=peer_id(me, other),
             device_id_type=MESH,
         )
 
-    for step in steps:
-        f_copy(p, to[step], step).start()
-    f_forward(p, 0, core).start()
+    for row in (0, 1):
+        f_copy(p, 1 + row, 1 + row, row).start()
+    for row in (0, 1):
+        f_copy(p, 2 - row, 2 - row, row).start()
+    for row in (0, 1):
+        f_forward(0, core, row).start()
     own_f = pltpu.make_async_copy(y.at[final_slot, own], fall.at[p, core], local_sem.at[1])
     own_f.start()
     one_step(DEG + 1, True)
@@ -304,14 +325,29 @@
         lax.fori_loop(0, owners, send, 0)
 
     strip(p, core)
-    f_forward(p, 0, other).wait_recv()
+    for row in (0, 1):
+        f_forward(0, other, row).wait_recv()
+    for row, (step, via) in enumerate(relays):
+        f_copy(side_of[step], step, step, row).wait_recv()
+        f_copy(side_of[step], via, 3, row).start()
+        f_forward(step, core, row).start()
     strip(p, other)
-    for step in steps:
-        f_copy(source_of[step], p, step).wait_recv()
-        f_forward(source_of[step], step, core).start()
-        strip(source_of[step], core)
-        f_forward(source_of[step], step, other).wait_recv()
-        strip(source_of[step], other)
+    for row, (step, via) in enumerate(relays):
+        f_copy(side_of[via], via, via, row).wait_recv()
+        f_forward(via, core, row).start()
+    strip(side_of[1], core)
+    strip(side_of[2], core)
+    for step in (1, 2):
+        for row in (0, 1):
+            f_forward(step, other, row).wait_recv()
+        strip(side_of[step], other)
+    for row in (0, 1):
+        f_copy(side_of[3], 3, 3, row).wait_recv()
+        f_forward(3, core, row).start()
+    strip(side_of[3], core)
+    for row in (0, 1):
+        f_forward(3, other, row).wait_recv()
+    strip(side_of[3], other)
     for source in range(group):
         filtered[:, source * wide : (source + 1) * wide] = fall[
             source, core, pl.ds(pl.multiple_of(p * rows_dev, two), rows_dev), :
@@ -340,12 +376,17 @@
         projected[:, source * wide : (source + 1) * wide] = summed[:, wide:]
 
     for step in steps:
-        h_copy(p, to[step], step).wait_send()
-        h_forward(source_of[step], step, core).wait_send()
-        v_copy(p, to[step], step).wait_send()
-        f_copy(p, to[step], step).wait_send()
-        f_forward(source_of[step], step, core).wait_send()
-    f_forward(p, 0, core).wait_send()
+        v_copy(p, side_of[step], step).wait_send()
+        for row in (0, 1):
+            h_forward(step, core, row).wait_send()
+            f_forward(step, core, row).wait_send()
+    for row, (step, via) in enumerate(relays):
+        for near in (1, 2):
+            h_copy(p, near, near, row).wait_send()
+            f_copy(p, near, near, row).wait_send()
+        h_copy(side_of[step], via, 3, row).wait_send()
+        f_copy(side_of[step], via, 3, row).wait_send()
+        f_forward(0, core, row).wait_send()
 
     def left_out(index, state):
         @pl.when(index != me)
@@ -388,7 +429,6 @@
         in_specs=[smem, smem, smem, vmem, vmem, vmem],
         out_specs=(vmem, vmem, vmem),
         scratch_shapes=[
-            pltpu.VMEM((pairs_dev, 2 * blk, 6 * blk), jnp.bfloat16),
             pltpu.VMEM((pairs_dev * GROUP, 2 * blk, 6 * blk), jnp.bfloat16),
             pltpu.VMEM((2, rows_slab + 4 * blk, wide), jnp.bfloat16),
             pltpu.VMEM((GROUP, cores, rows_slab, wide), jnp.bfloat16),
@@ -396,18 +436,18 @@
             pltpu.VMEM((count, piece, 2 * wide), jnp.bfloat16),
             pltpu.VMEM((count, piece, 2 * wide), jnp.bfloat16),
             dma((2,)),
-            dma((GROUP,)),
-            dma((GROUP,)),
-            dma((GROUP,)),
-            dma((GROUP,)),
+            dma((GROUP, 2)),
+            dma((GROUP, 2)),
+            dma((GROUP, 2)),
+            dma((GROUP, 2)),
             dma((GROUP,)),
             dma((GROUP,)),
             dma((2, 2)),
             dma((2, 2)),
-            dma((GROUP,)),
-            dma((GROUP,)),
-            dma((GROUP,)),
-            dma((GROUP,)),
+            dma((GROUP, 2)),
+            dma((GROUP, 2)),
+            dma((GROUP, 2)),
+            dma((GROUP, 2)),
             dma((count,)),
             dma((count,)),
         ],

time: 131 us -> 121 us (0.924)
  Pallas kernels: 123 us -> 113 us
    pallas_call x1, Pallas kernels: 123 us -> 113 us  [shards(): pl.pallas_call(functools.partial(kernel, dims), out_shape=(jax.ShapeDtype...]
where the time goes in v3:
time: 121 us
  Pallas kernels  113 us (93%)
  local copies, waits for them, and re-layouts  7.08 us (6%)
    pallas_call x1, Pallas kernels, shards(): pl.pallas_call(functools.partial(kernel, dims), out_shape=(jax.ShapeDtype...  113 us
    unnamed x15, local copies, waits for them, and re-layouts  7.08 us

profile of v3, /device:TPU:1, one launch (start us, length us, event | category | flops | bytes accessed | tf_op | source)
XLA Modules:
  0.0 120.8 jit_solution(8070185917131522464)
XLA Ops:
  0.6 0.0 copy-start
  0.6 1.0 copy-done
  1.7 0.0 copy-start.1
  1.7 1.0 copy-done.1
  2.7 0.0 copy-start.2
  2.7 0.9 copy-done.2
  3.6 0.0 copy-start.3
  3.6 0.7 copy-done.3
  4.3 0.0 copy-start.4
  4.3 0.7 copy-done.4
  5.0 0.0 copy-start.5
  5.0 0.7 copy-done.5
  5.6 113.0 %shard_map.85 = (bf16[512,512]{1,0:T(8,128)(2,1)S(1)}, f32[64,512]{1,0:T(8,128)S(1)}, f32[64,512]{1,0:T(8,128)S(1)}) custom-call(f32[42]{0:T(128)S(1)} %copy-done.5, s32[4,4]{1,0:T(4,128)S(1)} %copy-done.3, s32[4]{0:T(128)S(1)} %copy-done.4, bf16[512,512]{1,0:T(8,128)(2,1)S(1)} %copy-done, bf16[4,128,128]{2,1,0:T(8,128)(2,1)S(1)} %copy-done.2, ...), custom_call_target="tpu_custom_call" | custom-call | tf_op jit(solution)/shard_map/pallas_call | solution.py:422
  118.7 0.8 copy.12
  119.4 0.7 copy.13
  120.1 0.7 copy.14
Async XLA Ops:
  0.6 1.0 copy-start
  1.7 1.0 copy-start.1
  2.7 0.9 copy-start.2
  3.6 0.7 copy-start.3
  4.3 0.7 copy-start.4
  5.0 0.7 copy-start.5
